TPU v7x, 32 devices: a whole 2x2x4 slice. The times are simulated.
32 devices in a mesh: scene: 2 (over x), view: 16 (over z, y, core).
Axes of the slice: x: 2, y: 2, z: 4, core: 2. Of those that a mesh axis runs over, the one named last changes fastest.
Arguments:
- latents: bfloat16 [256, 64, 512], P(('scene', 'view')), parts along dimension 0, may hold values from -48 to 48
- norm_gain: float32 [512], replicated, may hold values from 0.1 to 1.9
- norm_shift: float32 [512], replicated, may hold values from -3 to 3
- w_first: bfloat16 [512, 3, 3, 512], replicated, may hold values from -0.09375 to 0.09375
- bias_first: float32 [512], replicated, may hold values from -3 to 3
- w_second: bfloat16 [512, 3, 3, 512], replicated, may hold values from -0.09375 to 0.09375
- bias_second: float32 [512], replicated, may hold values from -3 to 3
Outputs:
- decoded: bfloat16 [512, 128, 512], P(('scene', 'view')), parts along dimension 0
There are 2 independent parts, one for each index of `scene`. A program takes and returns all parts, laid end to end along the dimension named above; an argument that names none is the same for every part. Nothing has to cross between parts.
All inputs are finite; a program needn't handle non-finite values.
Results may differ from a plain program's by a relative error of at most 0.0051.
Values may be sent and summed in bfloat16 or wider, within the bound.
A program may use at most 128 MiB of HBM per device.

v0:
```python
import functools

import jax
import jax.numpy as jnp
from jax import lax
from jax.experimental import pallas as pl
from jax.experimental.pallas import tpu as pltpu
from jax.sharding import PartitionSpec as P

GROUPS = 32
H_LAT = 32
EPSILON = 1e-06
LANES = 128
F32 = jnp.float32
BF16 = jnp.bfloat16


def dot_nt(x, w):
    return lax.dot_general(x, w, (((1,), (1,)), ((), ())), preferred_element_type=F32)


def kernel(
    n_view, rows, cols, chans,
    lat_hbm, gain_ref, shift_ref, w1_hbm, b1_ref, w2_hbm, b2_ref,
    out_ref,
    lat, w1, w2, fold, act, acc, lhs_m, lhs_u, part, wide, stat, stat_in,
    lat_sem, w1_sem, w2_sem, halo_send, halo_recv, stat_send, stat_recv,
):
    me = lax.axis_index("view")
    slabs = H_LAT // rows
    views = n_view // slabs
    slab = me // views
    own = rows * cols
    has_up = slab > 0
    has_down = slab < slabs - 1

    own_copy = pltpu.make_async_copy(lat_hbm, lat.at[pl.ds(2, rows)], lat_sem)
    own_copy.start()

    barrier = pltpu.get_barrier_semaphore()

    def greet(k, carry):
        pl.semaphore_signal(barrier, inc=1, device_id={"view": lax.rem(me + k, n_view)})
        return carry

    lax.fori_loop(1, n_view, greet, 0, unroll=n_view <= 16)

    def w1_copy(t):
        return pltpu.make_async_copy(w1_hbm.at[t], w1.at[:, pl.ds(t * chans, chans)], w1_sem.at[t])

    def w2_copy(t):
        return pltpu.make_async_copy(w2_hbm.at[t], w2.at[t], w2_sem.at[t])

    for t in range(9):
        w1_copy(t).start()
    for t in range(9):
        w2_copy(t).start()

    own_copy.wait()

    def add_row(i, carry):
        x = lat[2 + i].astype(F32).reshape(cols // 8, 8, chans)
        return carry[0] + jnp.sum(x, axis=0), carry[1] + jnp.sum(x * x, axis=0)

    zero = jnp.zeros((8, chans), F32)
    sums, squares = lax.fori_loop(0, rows, add_row, (zero, zero))
    sums = jnp.sum(sums, axis=0, keepdims=True)
    squares = jnp.sum(squares, axis=0, keepdims=True)
    blocks = chans // LANES
    packed = jnp.concatenate(
        [v[:, k * LANES : (k + 1) * LANES] for v in (sums, squares) for k in range(blocks)], axis=0
    )
    lane = lax.broadcasted_iota(jnp.int32, packed.shape, 1)
    step = 1
    while step < chans // GROUPS:
        packed = packed + jnp.where(
            (lane & step) == 0,
            pltpu.roll(packed, LANES - step, 1),
            pltpu.roll(packed, step, 1),
        )
        step *= 2
    stat[...] = packed

    pl.semaphore_wait(barrier, n_view - 1)

    def stat_copy(k):
        return pltpu.make_async_remote_copy(
            src_ref=stat, dst_ref=stat_in.at[k - 1], send_sem=stat_send, recv_sem=stat_recv,
            device_id={"view": lax.rem(me + k, n_view)},
        )

    def send_stat(k, carry):
        stat_copy(k).start()
        return carry

    lax.fori_loop(1, n_view, send_stat, 0, unroll=n_view <= 16)

    up_copy = pltpu.make_async_remote_copy(
        src_ref=lat_hbm.at[pl.ds(0, 2)], dst_ref=lat.at[pl.ds(rows + 2, 2)],
        send_sem=halo_send.at[0], recv_sem=halo_recv.at[0],
        device_id={"view": jnp.maximum(me - views, 0)},
    )
    down_copy = pltpu.make_async_remote_copy(
        src_ref=lat_hbm.at[pl.ds(rows - 2, 2)], dst_ref=lat.at[pl.ds(0, 2)],
        send_sem=halo_send.at[1], recv_sem=halo_recv.at[1],
        device_id={"view": jnp.minimum(me + views, n_view - 1)},
    )

    @pl.when(has_up)
    def _():
        up_copy.start()

    @pl.when(has_down)
    def _():
        down_copy.start()

    for t in range(9):
        w2_copy(t).wait()
    piece = 32

    def fold_piece(k, carry):
        at = pl.ds(pl.multiple_of(k * piece, piece), piece)
        w = [w2[t, at].astype(F32) for t in range(9)]
        by_col = [w[s] + w[3 + s] + w[6 + s] for s in range(3)]
        fold[0, at] = (by_col[0] + by_col[1] + by_col[2]).astype(BF16)
        fold[1, at] = by_col[0].astype(BF16)
        fold[2, at] = by_col[2].astype(BF16)
        fold[3, at] = (w[0] + w[1] + w[2]).astype(BF16)
        fold[4, at] = (w[6] + w[7] + w[8]).astype(BF16)
        return carry

    lax.fori_loop(0, chans // piece, fold_piece, 0)

    pltpu.make_async_copy(stat_in, stat_in, stat_recv).wait()

    total = stat[...]
    total = total + jnp.sum(stat_in[...], axis=0)
    entries = float(own * (chans // GROUPS) * n_view)
    mean = total[:blocks] / entries
    var = total[blocks:] / entries - mean * mean
    inv = lax.rsqrt(var + EPSILON)

    def one_row(v):
        return jnp.concatenate([v[k : k + 1] for k in range(blocks)], axis=1)

    scale = one_row(inv) * gain_ref[...]
    offset = shift_ref[...] - one_row(mean) * scale

    col = lax.broadcasted_iota(jnp.int32, (cols, chans), 0)

    def left_of(x):
        return jnp.where(col == 0, 0.0, pltpu.roll(x, 1, 0))

    def right_of(x):
        return jnp.where(col == cols - 1, 0.0, pltpu.roll(x, cols - 1, 0))

    half_scale = scale * 0.5
    half_offset = offset * 0.5

    def activate(i, carry):
        h = lat[i].astype(F32) * half_scale + half_offset
        a = h + h * jnp.tanh(h)
        place = slab * rows + i - 2
        a = jnp.where(jnp.logical_and(place >= 0, place < H_LAT), a, 0.0)
        at = pl.ds(pl.multiple_of(i * cols, cols), cols)
        act[at, pl.ds(0, chans)] = left_of(a).astype(BF16)
        act[at, pl.ds(chans, chans)] = a.astype(BF16)
        act[at, pl.ds(2 * chans, chans)] = right_of(a).astype(BF16)
        return carry

    lax.fori_loop(2, rows + 2, activate, 0)
    for t in range(9):
        w1_copy(t).wait()
    deep = 3 * chans
    half = 256

    def taps(windows, n):
        lanes = pl.ds(n * half, half)
        terms = [
            dot_nt(
                jnp.concatenate([act[pl.ds(first + r * cols, size)] for first, size in windows], axis=0),
                w1[lanes, pl.ds(r * deep, deep)],
            )
            for r in range(3)
        ]
        return terms[0] + terms[1] + terms[2]

    for n in range(chans // half):
        acc[pl.ds(2 * cols, own - 2 * cols), pl.ds(n * half, half)] = taps([(2 * cols, own - 2 * cols)], n)

    @pl.when(has_up)
    def _():
        down_copy.wait_recv()

    @pl.when(has_down)
    def _():
        up_copy.wait_recv()

    lax.fori_loop(0, 2, activate, 0)
    lax.fori_loop(rows + 2, rows + 4, activate, 0)
    ends = [(0, 2 * cols), (own, 2 * cols)]
    for n in range(chans // half):
        term = taps(ends, n)
        for k, (first, size) in enumerate(ends):
            acc[pl.ds(first, size), pl.ds(n * half, half)] = term[k * size : (k + 1) * size]

    bias1 = b1_ref[...]

    def mixed_row(i):
        at = pl.ds(pl.multiple_of(i * cols, cols), cols)
        m = lat[i + 1].astype(F32) + acc[at] + bias1
        m = m.astype(BF16).astype(F32)
        place = slab * rows + i - 1
        return jnp.where(jnp.logical_and(place >= 0, place < H_LAT), m, 0.0)

    def spread(i, carry):
        m = mixed_row(i + 1)
        u = m - mixed_row(i)
        at = pl.ds(pl.multiple_of(i * cols, cols), cols)
        for ref, x in ((lhs_m, m), (lhs_u, u)):
            ref[0, at] = x.astype(BF16)
            ref[1, at] = (left_of(x) - x).astype(BF16)
            ref[2, at] = (right_of(x) - x).astype(BF16)
        return carry

    lax.fori_loop(0, rows + 1, spread, 0)

    width = 256

    for n in range(chans // width):
        lanes = pl.ds(n * width, width)
        head = pl.ds(0, own)
        base = dot_nt(lhs_m[0, head], fold[0, lanes]) + b2_ref[:, lanes]
        part[0] = base + dot_nt(lhs_m[1, head], fold[1, lanes])
        part[1] = base + dot_nt(lhs_m[2, head], fold[2, lanes])
        for p in range(2):
            at = pl.ds(p * cols, own)
            rise = dot_nt(lhs_u[0, at], fold[3 + p, lanes])
            for q in range(2):
                term = rise + dot_nt(lhs_u[1 + q, at], w2[6 * p + 2 * q, lanes])
                value = part[q] + term if p else part[q] - term
                for g in range(width // LANES):
                    wide[g, pl.ds(p * own * 2 + q, own, 2), :] = value[:, g * LANES : (g + 1) * LANES]
            for g in range(width // LANES):
                tile = wide[g, pl.ds(p * own * 2, own * 2), :].astype(BF16)
                out_ref[:, p, :, pl.ds(n * width + g * LANES, LANES)] = tile.reshape(rows, 2 * cols, LANES)

    pltpu.make_async_copy(stat_in, stat_in, stat_send).wait()

    @pl.when(has_up)
    def _():
        up_copy.wait_send()

    @pl.when(has_down)
    def _():
        down_copy.wait_send()


def per_device(n_view, latents, norm_gain, norm_shift, w_first, bias_first, w_second, bias_second):
    rows, cols, chans = latents.shape
    own = rows * cols
    flat = lambda w: jnp.transpose(w, (1, 2, 0, 3)).reshape(9, chans, chans)
    row = lambda v: v.reshape(1, chans)
    vmem = pl.BlockSpec(memory_space=pltpu.VMEM)
    hbm = pl.BlockSpec(memory_space=pl.ANY)
    out = pl.pallas_call(
        functools.partial(kernel, n_view, rows, cols, chans),
        out_shape=pltpu.VMEM((rows, 2, 2 * cols, chans), BF16),
        in_specs=[hbm, vmem, vmem, hbm, vmem, hbm, vmem],
        out_specs=vmem,
        scratch_shapes=[
            pltpu.VMEM((rows + 4, cols, chans), BF16),
            pltpu.VMEM((chans, 9 * chans), BF16),
            pltpu.VMEM((9, chans, chans), BF16),
            pltpu.VMEM((5, chans, chans), BF16),
            pltpu.VMEM(((rows + 4) * cols, 3 * chans), BF16),
            pltpu.VMEM(((rows + 2) * cols, chans), F32),
            pltpu.VMEM((3, own + cols, chans), BF16),
            pltpu.VMEM((3, own + cols, chans), BF16),
            pltpu.VMEM((2, own, 256), F32),
            pltpu.VMEM((2, own * 4, LANES), F32),
            pltpu.VMEM((2 * chans // LANES, LANES), F32),
            pltpu.VMEM((n_view - 1, 2 * chans // LANES, LANES), F32),
            pltpu.SemaphoreType.DMA,
            pltpu.SemaphoreType.DMA((9,)),
            pltpu.SemaphoreType.DMA((9,)),
            pltpu.SemaphoreType.DMA((2,)),
            pltpu.SemaphoreType.DMA((2,)),
            pltpu.SemaphoreType.DMA,
            pltpu.SemaphoreType.DMA,
        ],
        compiler_params=pltpu.CompilerParams(
            collective_id=0, has_side_effects=True, vmem_limit_bytes=60 * 1024 * 1024
        ),
    )(
        latents, row(norm_gain), row(norm_shift), flat(w_first), row(bias_first), flat(w_second),
        row(bias_second),
    )
    return out.reshape(2 * rows, 2 * cols, chans)


def solution(mesh):
    placed = (P(("scene", "view"), None, None), P(), P(), P(), P(), P(), P())
    return jax.shard_map(
        functools.partial(per_device, mesh.shape["view"]),
        mesh=mesh,
        in_specs=placed,
        out_specs=P(("scene", "view"), None, None),
        check_vma=False,
    )
```

profile of v0, /device:TPU:0, one launch (start us, length us, event | category | flops | bytes accessed | tf_op | source)
XLA Modules:
  0.0 19.7 jit_solution(5809296929743224100)
XLA Ops:
  0.0 18.4 %shard_map.73 = bf16[8,2,128,512]{3,2,1,0:T(8,128)(2,1)S(1)} custom-call(bf16[8,64,512]{2,1,0:T(8,128)(2,1)} %lat_hbm.1, f32[1,512]{1,0:T(1,128)} %bitcast.14, f32[1,512]{1,0:T(1,128)} %bitcast.15, bf16[9,512,512]{2,1,0:T(8,128)(2,1)} %bitcast.12, f32[1,512]{1,0:T(1,128)} %bitcast.16, bf16[9,512,512]{2,1,0:T(8,128)(2,1)} %bitcast.13, f32[1,512]{1,0:T(1,128)} %bitcast.17), custom_call_target="tpu_custom_call" | custom-call | tf_op jit(solution)/shard_map/pallas_call | solution.py:266
  18.4 1.3 %copy.9 = bf16[16,128,512]{2,1,0:T(8,128)(2,1)} copy(bf16[16,128,512]{2,1,0:T(8,128)(2,1)S(1)} %bitcast.11) | data formatting | bytes 4194304
where the time goes:
time: 19.9 us; the launch traced here: 19.7 us
  Pallas kernels  18.4 us (92%)
  local copies, waits for them, and re-layouts  1.32 us (7%)
    pallas_call x1, Pallas kernels, per_device(): pl.pallas_call(functools.partial(kernel, n_view, rows, cols, chans), out_...  18.4 us
    unnamed x1, local copies, waits for them, and re-layouts  1.32 us

commit v1 on v0

v1 whole, which is shorter than its diff:
```python
import functools

import jax
import jax.numpy as jnp
from jax import lax
from jax.experimental import pallas as pl
from jax.experimental.pallas import tpu as pltpu
from jax.sharding import PartitionSpec as P

GROUPS = 32
H_LAT = 32
EPSILON = 1e-06
LANES = 128
TILE = 256
F32 = jnp.float32
BF16 = jnp.bfloat16


def dot_nt(x, w):
    return lax.dot_general(x, w, (((1,), (1,)), ((), ())), preferred_element_type=F32)


def dot_nn(x, w):
    return lax.dot_general(x, w, (((1,), (0,)), ((), ())), preferred_element_type=F32)


def kernel(
    n_view, rows, cols, chans,
    lat_hbm, gain_hbm, shift_hbm, w1_hbm, b1_hbm, w2_hbm, b2_hbm,
    out_ref,
    lat, small, w1, gt, w2, fold, act, vbuf, mbuf, mx, lhs_m, lhs_u, part, wide, stat, stat_in,
    lat_sem, small_sem, w1_sem, w2_sem, halo_send, halo_recv, stat_send, stat_recv,
):
    me = lax.axis_index("view")
    slabs = H_LAT // rows
    views = n_view // slabs
    slab = me // views
    own = rows * cols
    has_up = slab > 0
    has_down = slab < slabs - 1

    barrier = pltpu.get_barrier_semaphore()

    def greet(k, carry):
        pl.semaphore_signal(barrier, inc=1, device_id={"view": lax.rem(me + k, n_view)})
        return carry

    def lat_copy(i):
        return pltpu.make_async_copy(lat_hbm.at[i], lat.at[2 + i], lat_sem.at[i])

    def small_copy(i):
        ref = (gain_hbm, shift_hbm, b1_hbm, b2_hbm)[i]
        return pltpu.make_async_copy(ref, small.at[i], small_sem.at[i])

    def w1_copy(t):
        return pltpu.make_async_copy(w1_hbm.at[t], w1.at[t], w1_sem.at[t])

    def w2_copy(t):
        return pltpu.make_async_copy(w2_hbm.at[t], w2.at[t], w2_sem.at[t])

    for i in range(rows):
        lat_copy(i).start()
    lax.fori_loop(1, n_view, greet, 0, unroll=n_view <= 16)
    for t in range(9):
        w1_copy(t).start()
    for i in range(4):
        small_copy(i).start()
    for t in range(9):
        w2_copy(t).start()

    sums = jnp.zeros((8, chans), F32)
    squares = jnp.zeros((8, chans), F32)
    for i in range(rows):
        lat_copy(i).wait()
        x = lat[2 + i].astype(F32).reshape(cols // 8, 8, chans)
        sums = sums + jnp.sum(x, axis=0)
        squares = squares + jnp.sum(x * x, axis=0)
    sums = jnp.sum(sums, axis=0, keepdims=True)
    squares = jnp.sum(squares, axis=0, keepdims=True)
    blocks = chans // LANES
    stat[...] = jnp.concatenate(
        [v[:, k * LANES : (k + 1) * LANES] for v in (sums, squares) for k in range(blocks)], axis=0
    )

    pl.semaphore_wait(barrier, n_view - 1)

    def send_stat(k, carry):
        to = k + (k >= me).astype(jnp.int32)
        slot = lax.rem(to - me + n_view, n_view) - 1
        pltpu.make_async_remote_copy(
            src_ref=stat, dst_ref=stat_in.at[slot], send_sem=stat_send, recv_sem=stat_recv,
            device_id={"view": to},
        ).start()
        return carry

    lax.fori_loop(0, n_view - 1, send_stat, 0, unroll=n_view <= 16)

    up_copy = pltpu.make_async_remote_copy(
        src_ref=lat.at[pl.ds(2, 2)], dst_ref=lat.at[pl.ds(rows + 2, 2)],
        send_sem=halo_send.at[0], recv_sem=halo_recv.at[0],
        device_id={"view": jnp.maximum(me - views, 0)},
    )
    down_copy = pltpu.make_async_remote_copy(
        src_ref=lat.at[pl.ds(rows, 2)], dst_ref=lat.at[pl.ds(0, 2)],
        send_sem=halo_send.at[1], recv_sem=halo_recv.at[1],
        device_id={"view": jnp.minimum(me + views, n_view - 1)},
    )

    @pl.when(has_up)
    def _():
        up_copy.start()

    @pl.when(has_down)
    def _():
        down_copy.start()

    tiles = chans // TILE
    eye = (
        lax.broadcasted_iota(jnp.int32, (TILE, TILE), 0) == lax.broadcasted_iota(jnp.int32, (TILE, TILE), 1)
    ).astype(F32).astype(BF16)
    for t in range(9):
        w1_copy(t).wait()

    def prepare(j, carry):
        k_at = pl.ds(pl.multiple_of(j // tiles * TILE, TILE), TILE)
        n_at = pl.ds(pl.multiple_of(lax.rem(j, tiles) * TILE, TILE), TILE)
        for s in range(3):
            g = [w1[3 * r + s, n_at, k_at] for r in range(3)]
            gt[0, s, k_at, n_at] = dot_nt(eye, g[0]).astype(BF16)
            gt[3, s, k_at, n_at] = dot_nt(eye, g[2]).astype(BF16)
            h = [v.astype(F32) for v in g]
            even = (h[0] + h[2]) * 0.5
            odd = h[1] * 0.5
            gt[1, s, k_at, n_at] = (even + odd).astype(BF16).T
            gt[2, s, k_at, n_at] = (even - odd).astype(BF16).T
        return carry

    lax.fori_loop(0, tiles * tiles, prepare, 0)

    for t in range(9):
        w2_copy(t).wait()
    piece = 32

    def fold_piece(k, carry):
        at = pl.ds(pl.multiple_of(k * piece, piece), piece)
        w = [w2[t, at].astype(F32) for t in range(9)]
        by_col = [w[s] + w[3 + s] + w[6 + s] for s in range(3)]
        fold[0, at] = (by_col[0] + by_col[1] + by_col[2]).astype(BF16)
        fold[1, at] = by_col[0].astype(BF16)
        fold[2, at] = by_col[2].astype(BF16)
        fold[3, at] = (w[0] + w[1] + w[2]).astype(BF16)
        fold[4, at] = (w[6] + w[7] + w[8]).astype(BF16)
        return carry

    lax.fori_loop(0, chans // piece, fold_piece, 0)
    for i in range(4):
        small_copy(i).wait()

    same = (
        lax.broadcasted_iota(jnp.int32, (LANES, LANES), 0) // (chans // GROUPS)
        == lax.broadcasted_iota(jnp.int32, (LANES, LANES), 1) // (chans // GROUPS)
    ).astype(F32).astype(BF16)

    pltpu.make_async_copy(stat_in, stat_in, stat_recv).wait()

    total = stat[...] + jnp.sum(stat_in[...], axis=0)
    high = total.astype(BF16).astype(F32)
    rest = total - high
    middle = rest.astype(BF16).astype(F32)
    low = rest - middle
    parts = jnp.concatenate([high, middle, low, jnp.zeros_like(low)], axis=0).astype(BF16)
    sized = dot_nn(parts, same)
    n_stat = 2 * blocks
    total = sized[:n_stat] + sized[n_stat : 2 * n_stat] + sized[2 * n_stat : 3 * n_stat]
    entries = float(own * (chans // GROUPS) * n_view)
    mean = total[:blocks] / entries
    var = total[blocks:] / entries - mean * mean
    inv = lax.rsqrt(var + EPSILON)

    def one_row(v):
        return jnp.concatenate([v[k : k + 1] for k in range(blocks)], axis=1)

    scale = one_row(inv) * small[0]
    offset = small[1] - one_row(mean) * scale
    half_scale = scale * 0.5
    half_offset = offset * 0.5

    col = lax.broadcasted_iota(jnp.int32, (cols, chans), 0)

    def left_of(x):
        return jnp.where(col == 0, 0.0, pltpu.roll(x, 1, 0))

    def right_of(x):
        return jnp.where(col == cols - 1, 0.0, pltpu.roll(x, cols - 1, 0))

    def activate(i):
        h = lat[i].astype(F32) * half_scale + half_offset
        a = h + h * jnp.tanh(h)
        if i < 2:
            a = jnp.where(has_up, a, 0.0)
        if i >= rows + 2:
            a = jnp.where(has_down, a, 0.0)
        act[0, i] = left_of(a).astype(BF16)
        act[1, i] = a.astype(BF16)
        act[2, i] = right_of(a).astype(BF16)

    inner = list(range(1, rows // 2))
    outer = [0, rows // 2]
    place = {p: k for k, p in enumerate(inner + outer)}

    def combine(k, p):
        a, b = ((0, 2), (1, 2), (2, 1), (1, 3))[k]
        at = pl.ds(place[p] * cols, cols)
        for s in range(3):
            x, y = act[s, 2 * p + a], act[s, 2 * p + b]
            vbuf[k, s, at] = x + y if k == 1 else x - y

    def products(k, pairs):
        at = pl.ds(place[pairs[0]] * cols, len(pairs) * cols)
        terms = [dot_nn(vbuf[k, s, at], gt[k, s]) for s in range(3)]
        mbuf[k, at] = terms[0] + terms[1] + terms[2]

    for i in range(2, rows + 2):
        activate(i)
    for k in range(4):
        for p in inner:
            combine(k, p)
        products(k, inner)

    @pl.when(has_up)
    def _():
        down_copy.wait_recv()

    @pl.when(has_down)
    def _():
        up_copy.wait_recv()

    bias1 = small[2]

    def mix(i):
        p, odd = i // 2, i % 2
        at = pl.ds(place[p] * cols, cols)
        conv = mbuf[1, at] - mbuf[2, at] - mbuf[3, at] if odd else mbuf[0, at] + mbuf[1, at] + mbuf[2, at]
        m = lat[i + 1].astype(F32) + conv + bias1
        m = m.astype(BF16).astype(F32)
        if i == 0:
            m = jnp.where(has_up, m, 0.0)
        if i == rows + 1:
            m = jnp.where(has_down, m, 0.0)
        left, right = left_of(m), right_of(m)
        mx[0, i] = left.astype(BF16)
        mx[1, i] = m.astype(BF16)
        mx[2, i] = right.astype(BF16)
        if 1 <= i <= rows:
            at = pl.ds((i - 1) * cols, cols)
            lhs_m[0, at] = m.astype(BF16)
            lhs_m[1, at] = (left - m).astype(BF16)
            lhs_m[2, at] = (right - m).astype(BF16)

    def rise_of(j):
        at = pl.ds(j * cols, cols)
        left, m, right = [mx[s, j + 1].astype(F32) - mx[s, j].astype(F32) for s in range(3)]
        lhs_u[0, at] = m.astype(BF16)
        lhs_u[1, at] = (left - m).astype(BF16)
        lhs_u[2, at] = (right - m).astype(BF16)

    for i in (0, 1, rows + 2, rows + 3):
        activate(i)
    for k in range(4):
        for p in outer:
            combine(k, p)
        products(k, outer)
    for i in range(2, rows):
        mix(i)
    for j in range(2, rows - 1):
        rise_of(j)

    width = TILE
    bias2 = small[3]

    def level(n, pieces):
        lanes = pl.ds(n * width, width)
        lhs = [jnp.concatenate([lhs_m[s, pl.ds(a, b)] for a, b in pieces], axis=0) for s in range(3)]
        base = dot_nt(lhs[0], fold[0, lanes]) + bias2[:, n * width : (n + 1) * width]
        for q in range(2):
            both = base + dot_nt(lhs[1 + q], fold[1 + q, lanes])
            done = 0
            for a, b in pieces:
                part[n, q, pl.ds(a, b)] = both[done : done + b]
                done += b

    level(0, [(cols, own - 2 * cols)])
    for i in (0, 1, rows, rows + 1):
        mix(i)
    for j in (0, 1, rows - 1, rows):
        rise_of(j)
    level(0, [(0, cols), (own - cols, cols)])
    for n in range(chans // width):
        lanes = pl.ds(n * width, width)
        if n:
            level(n, [(0, own)])
        for p in range(2):
            at = pl.ds(p * cols, own)
            rise = dot_nt(lhs_u[0, at], fold[3 + p, lanes])
            for q in range(2):
                term = rise + dot_nt(lhs_u[1 + q, at], w2[6 * p + 2 * q, lanes])
                value = part[n, q] + term if p else part[n, q] - term
                for g in range(width // LANES):
                    wide[g, pl.ds(p * own * 2 + q, own, 2), :] = value[:, g * LANES : (g + 1) * LANES]
            for g in range(width // LANES):
                tile = wide[g, pl.ds(p * own * 2, own * 2), :].astype(BF16)
                out_ref[:, p, :, pl.ds(n * width + g * LANES, LANES)] = tile.reshape(rows, 2 * cols, LANES)

    pltpu.make_async_copy(stat_in, stat_in, stat_send).wait()

    @pl.when(has_up)
    def _():
        up_copy.wait_send()

    @pl.when(has_down)
    def _():
        down_copy.wait_send()


def per_device(n_view, latents, norm_gain, norm_shift, w_first, bias_first, w_second, bias_second):
    rows, cols, chans = latents.shape
    own = rows * cols
    flat = lambda w: jnp.transpose(w, (1, 2, 0, 3)).reshape(9, chans, chans)
    row = lambda v: v.reshape(1, chans)
    hbm = pl.BlockSpec(memory_space=pl.ANY)
    n_stat = 2 * chans // LANES
    out = pl.pallas_call(
        functools.partial(kernel, n_view, rows, cols, chans),
        out_shape=pltpu.VMEM((rows, 2, 2 * cols, chans), BF16),
        in_specs=[hbm] * 7,
        out_specs=pl.BlockSpec(memory_space=pltpu.VMEM),
        scratch_shapes=[
            pltpu.VMEM((rows + 4, cols, chans), BF16),
            pltpu.VMEM((4, 1, chans), F32),
            pltpu.VMEM((9, chans, chans), BF16),
            pltpu.VMEM((4, 3, chans, chans), BF16),
            pltpu.VMEM((9, chans, chans), BF16),
            pltpu.VMEM((5, chans, chans), BF16),
            pltpu.VMEM((3, rows + 4, cols, chans), BF16),
            pltpu.VMEM((4, 3, (rows // 2 + 1) * cols, chans), BF16),
            pltpu.VMEM((4, (rows // 2 + 1) * cols, chans), F32),
            pltpu.VMEM((3, rows + 2, cols, chans), BF16),
            pltpu.VMEM((3, own, chans), BF16),
            pltpu.VMEM((3, own + cols, chans), BF16),
            pltpu.VMEM((chans // TILE, 2, own, TILE), F32),
            pltpu.VMEM((TILE // LANES, own * 4, LANES), F32),
            pltpu.VMEM((n_stat, LANES), F32),
            pltpu.VMEM((n_view - 1, n_stat, LANES), F32),
            pltpu.SemaphoreType.DMA((rows,)),
            pltpu.SemaphoreType.DMA((4,)),
            pltpu.SemaphoreType.DMA((9,)),
            pltpu.SemaphoreType.DMA((9,)),
            pltpu.SemaphoreType.DMA((2,)),
            pltpu.SemaphoreType.DMA((2,)),
            pltpu.SemaphoreType.DMA,
            pltpu.SemaphoreType.DMA,
        ],
        compiler_params=pltpu.CompilerParams(
            collective_id=0, has_side_effects=True, vmem_limit_bytes=60 * 1024 * 1024
        ),
    )(
        latents, row(norm_gain), row(norm_shift), flat(w_first), row(bias_first), flat(w_second),
        row(bias_second),
    )
    return out.reshape(2 * rows, 2 * cols, chans)


def solution(mesh):
    placed = (P(("scene", "view"), None, None), P(), P(), P(), P(), P(), P())
    return jax.shard_map(
        functools.partial(per_device, mesh.shape["view"]),
        mesh=mesh,
        in_specs=placed,
        out_specs=P(("scene", "view"), None, None),
        check_vma=False,
    )
```

time: 19.9 us -> 17.5 us (0.88)
  Pallas kernels: 18.4 us -> 16.1 us
    pallas_call x1, Pallas kernels: 18.4 us -> 16.1 us  [per_device(): pl.pallas_call(functools.partial(kernel, n_view, rows, cols, chans), out_...]
where the time goes in v1:
time: 17.5 us; the launch traced here: 17.4 us
  Pallas kernels  16.1 us (92%)
  local copies, waits for them, and re-layouts  1.32 us (8%)
    pallas_call x1, Pallas kernels, per_device(): pl.pallas_call(functools.partial(kernel, n_view, rows, cols, chans), out_...  16.1 us
    unnamed x1, local copies, waits for them, and re-layouts  1.32 us

profile of v1, /device:TPU:0, one launch (start us, length us, event | category | flops | bytes accessed | tf_op | source)
XLA Modules:
  0.0 17.4 jit_solution(449193956236060016)
XLA Ops:
  0.0 16.1 %shard_map.73 = bf16[8,2,128,512]{3,2,1,0:T(8,128)(2,1)S(1)} custom-call(bf16[8,64,512]{2,1,0:T(8,128)(2,1)} %lat_hbm.1, f32[1,512]{1,0:T(1,128)} %bitcast.14, f32[1,512]{1,0:T(1,128)} %bitcast.15, bf16[9,512,512]{2,1,0:T(8,128)(2,1)} %bitcast.12, f32[1,512]{1,0:T(1,128)} %bitcast.16, bf16[9,512,512]{2,1,0:T(8,128)(2,1)} %bitcast.13, f32[1,512]{1,0:T(1,128)} %bitcast.17), custom_call_target="tpu_custom_call" | custom-call | tf_op jit(solution)/shard_map/pallas_call | solution.py:332
  16.1 1.3 %copy.9 = bf16[16,128,512]{2,1,0:T(8,128)(2,1)} copy(bf16[16,128,512]{2,1,0:T(8,128)(2,1)S(1)} %bitcast.11) | data formatting | bytes 4194304

commit v2 on v1

v2 whole, which is shorter than its diff:
```python
import functools

import jax
import jax.numpy as jnp
from jax import lax
from jax.experimental import pallas as pl
from jax.experimental.pallas import tpu as pltpu
from jax.sharding import PartitionSpec as P

GROUPS = 32
H_LAT = 32
EPSILON = 1e-06
LANES = 128
TILE = 256
F32 = jnp.float32
BF16 = jnp.bfloat16


def dot_nt(x, w):
    return lax.dot_general(x, w, (((1,), (1,)), ((), ())), preferred_element_type=F32)


def dot_nn(x, w):
    return lax.dot_general(x, w, (((1,), (0,)), ((), ())), preferred_element_type=F32)


def kernel(
    n_view, rows, cols, chans,
    lat_hbm, gain_hbm, shift_hbm, w1_hbm, b1_hbm, w2_hbm, b2_hbm,
    out_ref,
    lat, small, w1, gt, w2, fold, act, vbuf, mbuf, mx, lhs_u, part, wide, stat, stat_in,
    lat_sem, small_sem, w1_sem, w2_sem, halo_send, halo_recv, stat_send, stat_recv,
):
    me = lax.axis_index("view")
    slabs = H_LAT // rows
    views = n_view // slabs
    slab = me // views
    own = rows * cols
    has_up = slab > 0
    has_down = slab < slabs - 1

    barrier = pltpu.get_barrier_semaphore()

    def greet(k, carry):
        pl.semaphore_signal(barrier, inc=1, device_id={"view": lax.rem(me + k, n_view)})
        return carry

    lat_rows = rows // 4

    def lat_copy(i):
        some = pl.ds(i * lat_rows, lat_rows)
        return pltpu.make_async_copy(lat_hbm.at[some], lat.at[pl.ds(2 + i * lat_rows, lat_rows)], lat_sem.at[i])

    def small_copy(i):
        ref = (gain_hbm, shift_hbm, b1_hbm, b2_hbm)[i]
        return pltpu.make_async_copy(ref, small.at[i], small_sem)

    def w1_copy(t):
        return pltpu.make_async_copy(w1_hbm.at[t], w1.at[t], w1_sem.at[t // 5])

    def w2_copy(t):
        return pltpu.make_async_copy(w2_hbm.at[t], w2.at[t], w2_sem)

    for i in range(4):
        lat_copy(i).start()
    lax.fori_loop(1, n_view, greet, 0, unroll=n_view <= 16)
    for t in range(9):
        w1_copy(t).start()
    for i in range(4):
        small_copy(i).start()

    tiles = chans // TILE
    eye = (
        lax.broadcasted_iota(jnp.int32, (TILE, TILE), 0) == lax.broadcasted_iota(jnp.int32, (TILE, TILE), 1)
    ).astype(F32).astype(BF16)

    def prepare(j, carry):
        k0 = pl.multiple_of(j // tiles * TILE, TILE)
        n0 = pl.multiple_of(lax.rem(j, tiles) * TILE, TILE)
        for s in range(3):
            for k, r in ((0, 0), (3, 2)):
                g = w1[3 * r + s, pl.ds(n0, TILE), pl.ds(k0, TILE)]
                gt[k, s, pl.ds(k0, TILE), pl.ds(n0, TILE)] = dot_nt(eye, g).astype(BF16)
            for a in range(0, TILE, LANES):
                for b in range(0, TILE, LANES):
                    n_at, k_at = pl.ds(n0 + a, LANES), pl.ds(k0 + b, LANES)
                    h = [w1[3 * r + s, n_at, k_at].astype(F32) for r in range(3)]
                    even = (h[0] + h[2]) * 0.5
                    odd = h[1] * 0.5
                    gt[1, s, k_at, n_at] = (even + odd).astype(BF16).T
                    gt[2, s, k_at, n_at] = (even - odd).astype(BF16).T
        return carry

    def prepare_all():
        pltpu.make_async_copy(w1.at[pl.ds(0, 5)], w1.at[pl.ds(0, 5)], w1_sem.at[0]).wait()
        for t in range(9):
            w2_copy(t).start()
        pltpu.make_async_copy(w1.at[pl.ds(5, 4)], w1.at[pl.ds(5, 4)], w1_sem.at[1]).wait()
        lax.fori_loop(0, tiles * tiles, prepare, 0)

    sums = jnp.zeros((8, chans), F32)
    squares = jnp.zeros((8, chans), F32)
    for i in range(rows):
        if i % lat_rows == 0:
            lat_copy(i // lat_rows).wait()
        x = lat[2 + i].astype(F32).reshape(cols // 8, 8, chans)
        sums = sums + jnp.sum(x, axis=0)
        squares = squares + jnp.sum(x * x, axis=0)
    sums = jnp.sum(sums, axis=0, keepdims=True)
    squares = jnp.sum(squares, axis=0, keepdims=True)
    blocks = chans // LANES
    stat[...] = jnp.concatenate(
        [v[:, k * LANES : (k + 1) * LANES] for v in (sums, squares) for k in range(blocks)], axis=0
    )

    @pl.when(jnp.logical_not(has_up))
    def _():
        prepare_all()

    pl.semaphore_wait(barrier, n_view - 1)

    def send_stat(k, carry):
        to = k + (k >= me).astype(jnp.int32)
        slot = lax.rem(to - me + n_view, n_view) - 1
        pltpu.make_async_remote_copy(
            src_ref=stat, dst_ref=stat_in.at[slot], send_sem=stat_send, recv_sem=stat_recv,
            device_id={"view": to},
        ).start()
        return carry

    lax.fori_loop(0, n_view - 1, send_stat, 0, unroll=n_view <= 16)

    up_copy = pltpu.make_async_remote_copy(
        src_ref=lat.at[pl.ds(2, 2)], dst_ref=lat.at[pl.ds(rows + 2, 2)],
        send_sem=halo_send.at[0], recv_sem=halo_recv.at[0],
        device_id={"view": jnp.maximum(me - views, 0)},
    )
    down_copy = pltpu.make_async_remote_copy(
        src_ref=lat.at[pl.ds(rows, 2)], dst_ref=lat.at[pl.ds(0, 2)],
        send_sem=halo_send.at[1], recv_sem=halo_recv.at[1],
        device_id={"view": jnp.minimum(me + views, n_view - 1)},
    )

    @pl.when(has_up)
    def _():
        up_copy.start()

    @pl.when(has_down)
    def _():
        down_copy.start()

    @pl.when(has_up)
    def _():
        prepare_all()

    pltpu.make_async_copy(w2, w2, w2_sem).wait()

    def fold_tile(j, carry):
        k0 = pl.multiple_of(j // tiles * TILE, TILE)
        n0 = pl.multiple_of(lax.rem(j, tiles) * TILE, TILE)
        for k, t in enumerate((0, 2, 6, 8)):
            g = w2[t, pl.ds(n0, TILE), pl.ds(k0, TILE)]
            fold[5 + k, pl.ds(k0, TILE), pl.ds(n0, TILE)] = dot_nt(eye, g).astype(BF16)
        for a in range(0, TILE, LANES):
            for b in range(0, TILE, LANES):
                n_at, k_at = pl.ds(n0 + a, LANES), pl.ds(k0 + b, LANES)

                def add(*taps):
                    terms = [w2[t, n_at, k_at].astype(F32) for t in taps]
                    return terms[0] + terms[1] + terms[2]

                def put(i, v):
                    fold[i, k_at, n_at] = v.astype(BF16).T

                put(3, add(0, 1, 2))
                put(4, add(6, 7, 8))
                left = add(0, 3, 6)
                put(1, left)
                right = add(2, 5, 8)
                put(2, right)
                put(0, left + add(1, 4, 7) + right)
        return carry

    lax.fori_loop(0, tiles * tiles, fold_tile, 0)
    pltpu.make_async_copy(small, small, small_sem).wait()

    same = (
        lax.broadcasted_iota(jnp.int32, (LANES, LANES), 0) // (chans // GROUPS)
        == lax.broadcasted_iota(jnp.int32, (LANES, LANES), 1) // (chans // GROUPS)
    ).astype(F32).astype(BF16)

    pltpu.make_async_copy(stat_in, stat_in, stat_recv).wait()

    total = stat[...] + jnp.sum(stat_in[...], axis=0)
    high = total.astype(BF16).astype(F32)
    rest = total - high
    middle = rest.astype(BF16).astype(F32)
    low = rest - middle
    parts = jnp.concatenate([high, middle, low, jnp.zeros_like(low)], axis=0).astype(BF16)
    sized = dot_nn(parts, same)
    n_stat = 2 * blocks
    total = sized[:n_stat] + sized[n_stat : 2 * n_stat] + sized[2 * n_stat : 3 * n_stat]
    entries = float(own * (chans // GROUPS) * n_view)
    mean = total[:blocks] / entries
    var = total[blocks:] / entries - mean * mean
    inv = lax.rsqrt(var + EPSILON)

    def one_row(v):
        return jnp.concatenate([v[k : k + 1] for k in range(blocks)], axis=1)

    scale = one_row(inv) * small[0]
    offset = small[1] - one_row(mean) * scale
    half_scale = scale * 0.5
    half_offset = offset * 0.5

    groups = range(chans // LANES)
    first_row = lax.broadcasted_iota(jnp.int32, (8, LANES), 0)

    def left_of(x):
        y = pltpu.roll(x, 1, 0)
        return jnp.concatenate([jnp.where(first_row == 0, 0.0, y[:8]), y[8:]], axis=0)

    def right_of(x):
        y = pltpu.roll(x, cols - 1, 0)
        return jnp.concatenate([y[:-8], jnp.where(first_row == 7, 0.0, y[-8:])], axis=0)

    def activate(i):
        for g in groups:
            lanes = pl.ds(g * LANES, LANES)
            side = slice(g * LANES, (g + 1) * LANES)
            h = lat[i, :, lanes].astype(F32) * half_scale[:, side] + half_offset[:, side]
            a = h + h * jnp.tanh(h)
            if i < 2:
                a = jnp.where(has_up, a, 0.0)
            if i >= rows + 2:
                a = jnp.where(has_down, a, 0.0)
            act[0, i, :, lanes] = left_of(a).astype(BF16)
            act[1, i, :, lanes] = a.astype(BF16)
            act[2, i, :, lanes] = right_of(a).astype(BF16)

    inner = list(range(1, rows // 2))
    outer = [0, rows // 2]
    place = {p: k for k, p in enumerate(inner + outer)}

    def arrange(k, pairs):
        a, b = ((0, 2), (1, 2), (2, 1), (1, 3))[k]
        for p in pairs:
            at = pl.ds(place[p] * cols, cols)
            for s in range(3):
                x, y = act[s, 2 * p + a], act[s, 2 * p + b]
                vbuf[k, s, at] = x + y if k == 1 else x - y

    def products(n, k, pairs):
        at = pl.ds(place[pairs[0]] * cols, len(pairs) * cols)
        lanes = pl.ds(n * TILE, TILE)
        terms = [dot_nn(vbuf[k, s, at], gt[k, s, :, lanes]) for s in range(3)]
        mbuf[k, at, lanes] = terms[0] + terms[1] + terms[2]

    bias1 = small[2]

    def mix(n, i):
        p, odd = i // 2, i % 2
        at = pl.ds(place[p] * cols, cols)
        for g in groups[n * TILE // LANES : (n + 1) * TILE // LANES]:
            lanes = pl.ds(g * LANES, LANES)
            v = [mbuf[k, at, lanes] for k in ((1, 2, 3) if odd else (0, 1, 2))]
            conv = v[0] - v[1] - v[2] if odd else v[0] + v[1] + v[2]
            m = lat[i + 1, :, lanes].astype(F32) + conv + bias1[:, g * LANES : (g + 1) * LANES]
            if i == 0:
                m = jnp.where(has_up, m, 0.0)
            if i == rows + 1:
                m = jnp.where(has_down, m, 0.0)
            narrow = m.astype(BF16)
            m = narrow.astype(F32)
            to = pl.ds(i * cols, cols)
            mx[0, to, lanes] = narrow
            mx[1, to, lanes] = left_of(m).astype(BF16) - narrow
            mx[2, to, lanes] = right_of(m).astype(BF16) - narrow

    def rise_of(n, j):
        lanes = pl.ds(n * TILE, TILE)
        here, below = pl.ds(j * cols, cols), pl.ds((j + 1) * cols, cols)
        for s in range(3):
            lhs_u[s, here, lanes] = mx[s, below, lanes] - mx[s, here, lanes]

    width = TILE
    bias2 = small[3]

    def take(ref, s, pieces):
        return jnp.concatenate([ref[s, pl.ds(a * cols, b * cols)] for a, b in pieces], axis=0)

    def level(n, pieces):
        lanes = pl.ds(n * width, width)
        mine = [(a + 1, b) for a, b in pieces]
        base = dot_nn(take(mx, 0, mine), fold[0, :, lanes]) + bias2[:, n * width : (n + 1) * width]
        for q in range(2):
            both = base + dot_nn(take(mx, 1 + q, mine), fold[1 + q, :, lanes])
            done = 0
            for a, b in pieces:
                part[n, q, pl.ds(a * cols, b * cols)] = both[done * cols : (done + b) * cols]
                done += b

    def finish(n, p, pieces):
        lanes = pl.ds(n * width, width)
        mine = [(a + p, b) for a, b in pieces]
        rise = dot_nn(take(lhs_u, 0, mine), fold[3 + p, :, lanes])
        for q in range(2):
            term = rise + dot_nn(take(lhs_u, 1 + q, mine), fold[5 + 2 * p + q, :, lanes])
            done = 0
            for a, b in pieces:
                for i in range(a, a + b):
                    for g in range(width // LANES):
                        x = part[n, q, pl.ds(i * cols, cols), pl.ds(g * LANES, LANES)]
                        y = term[done * cols : (done + 1) * cols, g * LANES : (g + 1) * LANES]
                        wide[g, pl.ds((p * rows + i) * 2 * cols + q, cols, 2), :] = x + y if p else x - y
                    done += 1
        for a, b in pieces:
            for i in range(a, a + b):
                for g in range(width // LANES):
                    tile = wide[g, pl.ds((p * rows + i) * 2 * cols, 2 * cols), :].astype(BF16)
                    out_ref[i, p, :, pl.ds(n * width + g * LANES, LANES)] = tile

    columns = range(chans // width)
    for i in range(2, rows + 2, 2):
        activate(i)
    arrange(0, inner)
    products(0, 0, inner)
    for i in range(3, rows + 2, 2):
        activate(i)
    for k in range(1, 4):
        arrange(k, inner)
        products(0, k, inner)
    for n in columns[1:]:
        for k in range(4):
            products(n, k, inner)
        for i in range(2, rows):
            mix(n - 1, i)
    for i in range(2, rows):
        mix(columns[-1], i)
    for n in columns:
        level(n, [(1, rows - 2)])
    for n in columns:
        for j in range(2, rows - 1):
            rise_of(n, j)

    @pl.when(has_up)
    def _():
        down_copy.wait_recv()

    @pl.when(has_down)
    def _():
        up_copy.wait_recv()

    for i in (0, 1, rows + 2, rows + 3):
        activate(i)
    for k in range(4):
        arrange(k, outer)
        products(0, k, outer)
    for n in columns[1:]:
        for k in range(4):
            products(n, k, outer)
        for i in (0, 1, rows, rows + 1):
            mix(n - 1, i)
    finish(0, 0, [(2, rows - 3)])
    for i in (0, 1, rows, rows + 1):
        mix(columns[-1], i)
    for n in columns:
        for j in (0, 1, rows - 1, rows):
            rise_of(n, j)
    for n in columns:
        level(n, [(0, 1), (rows - 1, 1)])
    finish(0, 0, [(0, 2), (rows - 1, 1)])
    finish(0, 1, [(0, rows)])
    for n in columns[1:]:
        finish(n, 0, [(0, rows)])
        for a in range(0, rows, rows // 4):
            finish(n, 1, [(a, rows // 4)])

    pltpu.make_async_copy(stat_in, stat_in, stat_send).wait()

    @pl.when(has_up)
    def _():
        up_copy.wait_send()

    @pl.when(has_down)
    def _():
        down_copy.wait_send()


def per_device(n_view, latents, norm_gain, norm_shift, w_first, bias_first, w_second, bias_second):
    rows, cols, chans = latents.shape
    own = rows * cols
    flat = lambda w: jnp.transpose(w, (1, 2, 0, 3)).reshape(9, chans, chans)
    row = lambda v: v.reshape(1, chans)
    hbm = pl.BlockSpec(memory_space=pl.ANY)
    n_stat = 2 * chans // LANES
    out = pl.pallas_call(
        functools.partial(kernel, n_view, rows, cols, chans),
        out_shape=pltpu.VMEM((rows, 2, 2 * cols, chans), BF16),
        in_specs=[hbm] * 7,
        out_specs=pl.BlockSpec(memory_space=pltpu.VMEM),
        scratch_shapes=[
            pltpu.VMEM((rows + 4, cols, chans), BF16),
            pltpu.VMEM((4, 1, chans), F32),
            pltpu.VMEM((9, chans, chans), BF16),
            pltpu.VMEM((4, 3, chans, chans), BF16),
            pltpu.VMEM((9, chans, chans), BF16),
            pltpu.VMEM((9, chans, chans), BF16),
            pltpu.VMEM((3, rows + 4, cols, chans), BF16),
            pltpu.VMEM((4, 3, (rows // 2 + 1) * cols, chans), BF16),
            pltpu.VMEM((4, (rows // 2 + 1) * cols, chans), F32),
            pltpu.VMEM((3, own + 2 * cols, chans), BF16),
            pltpu.VMEM((3, own + cols, chans), BF16),
            pltpu.VMEM((chans // TILE, 2, own, TILE), F32),
            pltpu.VMEM((TILE // LANES, own * 4, LANES), F32),
            pltpu.VMEM((n_stat, LANES), F32),
            pltpu.VMEM((n_view - 1, n_stat, LANES), F32),
            pltpu.SemaphoreType.DMA((4,)),
            pltpu.SemaphoreType.DMA,
            pltpu.SemaphoreType.DMA((2,)),
            pltpu.SemaphoreType.DMA,
            pltpu.SemaphoreType.DMA((2,)),
            pltpu.SemaphoreType.DMA((2,)),
            pltpu.SemaphoreType.DMA,
            pltpu.SemaphoreType.DMA,
        ],
        compiler_params=pltpu.CompilerParams(
            collective_id=0, has_side_effects=True, vmem_limit_bytes=60 * 1024 * 1024
        ),
    )(
        latents, row(norm_gain), row(norm_shift), flat(w_first), row(bias_first), flat(w_second),
        row(bias_second),
    )
    return out.reshape(2 * rows, 2 * cols, chans)


def solution(mesh):
    placed = (P(("scene", "view"), None, None), P(), P(), P(), P(), P(), P())
    return jax.shard_map(
        functools.partial(per_device, mesh.shape["view"]),
        mesh=mesh,
        in_specs=placed,
        out_specs=P(("scene", "view"), None, None),
        check_vma=False,
    )
```

time: 17.5 us -> 17 us (0.971)
  Pallas kernels: 16.1 us -> 15.5 us
    pallas_call x1, Pallas kernels: 16.1 us -> 15.5 us  [per_device(): pl.pallas_call(functools.partial(kernel, n_view, rows, cols, chans), out_...]
where the time goes in v2:
time: 17 us; the launch traced here: 16.8 us
  Pallas kernels  15.5 us (91%)
  local copies, waits for them, and re-layouts  1.32 us (8%)
    pallas_call x1, Pallas kernels, per_device(): pl.pallas_call(functools.partial(kernel, n_view, rows, cols, chans), out_...  15.5 us
    unnamed x1, local copies, waits for them, and re-layouts  1.32 us

profile of v2, /device:TPU:0, one launch (start us, length us, event | category | flops | bytes accessed | tf_op | source)
XLA Modules:
  0.0 16.8 jit_solution(12057435672269242415)
XLA Ops:
  0.0 15.5 %shard_map.73 = bf16[8,2,128,512]{3,2,1,0:T(8,128)(2,1)S(1)} custom-call(bf16[8,64,512]{2,1,0:T(8,128)(2,1)} %lat_hbm.1, f32[1,512]{1,0:T(1,128)} %bitcast.14, f32[1,512]{1,0:T(1,128)} %bitcast.15, bf16[9,512,512]{2,1,0:T(8,128)(2,1)} %bitcast.12, f32[1,512]{1,0:T(1,128)} %bitcast.16, bf16[9,512,512]{2,1,0:T(8,128)(2,1)} %bitcast.13, f32[1,512]{1,0:T(1,128)} %bitcast.17), custom_call_target="tpu_custom_call" | custom-call | tf_op jit(solution)/shard_map/pallas_call | solution.py:397
  15.5 1.3 %copy.9 = bf16[16,128,512]{2,1,0:T(8,128)(2,1)} copy(bf16[16,128,512]{2,1,0:T(8,128)(2,1)S(1)} %bitcast.11) | data formatting | bytes 4194304

commit v3 on v2

--- a/solution.py
+++ b/solution.py
@@ -141,13 +141,24 @@
         device_id={"view": jnp.minimum(me + views, n_view - 1)},
     )
 
+    own_up = pltpu.make_async_copy(lat_hbm.at[pl.ds(0, 2)], lat.at[pl.ds(0, 2)], halo_recv.at[1])
+    own_down = pltpu.make_async_copy(lat_hbm.at[pl.ds(0, 2)], lat.at[pl.ds(rows + 2, 2)], halo_recv.at[0])
+
     @pl.when(has_up)
     def _():
         up_copy.start()
 
+    @pl.when(jnp.logical_not(has_up))
+    def _():
+        own_up.start()
+
     @pl.when(has_down)
     def _():
         down_copy.start()
+
+    @pl.when(jnp.logical_not(has_down))
+    def _():
+        own_down.start()
 
     @pl.when(has_up)
     def _():
@@ -321,20 +332,22 @@
                     out_ref[i, p, :, pl.ds(n * width + g * LANES, LANES)] = tile
 
     columns = range(chans // width)
+
     for i in range(2, rows + 2, 2):
         activate(i)
     arrange(0, inner)
-    products(0, 0, inner)
+    for n in columns:
+        products(n, 0, inner)
     for i in range(3, rows + 2, 2):
         activate(i)
-    for k in range(1, 4):
-        arrange(k, inner)
-        products(0, k, inner)
-    for n in columns[1:]:
-        for k in range(4):
+    for n in columns:
+        for k in range(1, 4):
+            if n == 0:
+                arrange(k, inner)
             products(n, k, inner)
-        for i in range(2, rows):
-            mix(n - 1, i)
+        if n:
+            for i in range(2, rows):
+                mix(n - 1, i)
     for i in range(2, rows):
         mix(columns[-1], i)
     for n in columns:
@@ -343,24 +356,23 @@
         for j in range(2, rows - 1):
             rise_of(n, j)
 
-    @pl.when(has_up)
-    def _():
-        down_copy.wait_recv()
-
-    @pl.when(has_down)
-    def _():
-        up_copy.wait_recv()
-
-    for i in (0, 1, rows + 2, rows + 3):
+    own_up.wait()
+    own_down.wait()
+    for i in (0, rows + 2):
         activate(i)
-    for k in range(4):
-        arrange(k, outer)
-        products(0, k, outer)
-    for n in columns[1:]:
-        for k in range(4):
+    arrange(0, outer)
+    for n in columns:
+        products(n, 0, outer)
+    for i in (1, rows + 3):
+        activate(i)
+    for n in columns:
+        for k in range(1, 4):
+            if n == 0:
+                arrange(k, outer)
             products(n, k, outer)
-        for i in (0, 1, rows, rows + 1):
-            mix(n - 1, i)
+        if n:
+            for i in (0, 1, rows, rows + 1):
+                mix(n - 1, i)
     finish(0, 0, [(2, rows - 3)])
     for i in (0, 1, rows, rows + 1):
         mix(columns[-1], i)
@@ -373,8 +385,7 @@
     finish(0, 1, [(0, rows)])
     for n in columns[1:]:
         finish(n, 0, [(0, rows)])
-        for a in range(0, rows, rows // 4):
-            finish(n, 1, [(a, rows // 4)])
+        finish(n, 1, [(0, rows)])
 
     pltpu.make_async_copy(stat_in, stat_in, stat_send).wait()
 

time: 17 us -> 16.6 us (0.976)
  Pallas kernels: 15.5 us -> 15.1 us
    pallas_call x1, Pallas kernels: 15.5 us -> 15.1 us  [per_device(): pl.pallas_call(functools.partial(kernel, n_view, rows, cols, chans), out_...]
where the time goes in v3:
time: 16.6 us; the launch traced here: 16.4 us
  Pallas kernels  15.1 us (91%)
  local copies, waits for them, and re-layouts  1.32 us (8%)
    pallas_call x1, Pallas kernels, per_device(): pl.pallas_call(functools.partial(kernel, n_view, rows, cols, chans), out_...  15.1 us
    unnamed x1, local copies, waits for them, and re-layouts  1.32 us

profile of v3, /device:TPU:0, one launch (start us, length us, event | category | flops | bytes accessed | tf_op | source)
XLA Modules:
  0.0 16.4 jit_solution(16800487736781665407)
XLA Ops:
  0.0 15.1 %shard_map.73 = bf16[8,2,128,512]{3,2,1,0:T(8,128)(2,1)S(1)} custom-call(bf16[8,64,512]{2,1,0:T(8,128)(2,1)} %lat_hbm.1, f32[1,512]{1,0:T(1,128)} %bitcast.14, f32[1,512]{1,0:T(1,128)} %bitcast.15, bf16[9,512,512]{2,1,0:T(8,128)(2,1)} %bitcast.12, f32[1,512]{1,0:T(1,128)} %bitcast.16, bf16[9,512,512]{2,1,0:T(8,128)(2,1)} %bitcast.13, f32[1,512]{1,0:T(1,128)} %bitcast.17), custom_call_target="tpu_custom_call" | custom-call | tf_op jit(solution)/shard_map/pallas_call | solution.py:408
  15.1 1.3 %copy.9 = bf16[16,128,512]{2,1,0:T(8,128)(2,1)} copy(bf16[16,128,512]{2,1,0:T(8,128)(2,1)S(1)} %bitcast.11) | data formatting | bytes 4194304

commit v4 on v3

--- a/solution.py
+++ b/solution.py
@@ -28,7 +28,7 @@
     n_view, rows, cols, chans,
     lat_hbm, gain_hbm, shift_hbm, w1_hbm, b1_hbm, w2_hbm, b2_hbm,
     out_ref,
-    lat, small, w1, gt, w2, fold, act, vbuf, mbuf, mx, lhs_u, part, wide, stat, stat_in,
+    lat, small, w1, gt, w2, fold, act, vbuf, mbuf, mx, lhs_u, part, wide, edge, stat, stat_in,
     lat_sem, small_sem, w1_sem, w2_sem, halo_send, halo_recv, stat_send, stat_recv,
 ):
     me = lax.axis_index("view")
@@ -45,7 +45,7 @@
         pl.semaphore_signal(barrier, inc=1, device_id={"view": lax.rem(me + k, n_view)})
         return carry
 
-    lat_rows = rows // 4
+    lat_rows = 1
 
     def lat_copy(i):
         some = pl.ds(i * lat_rows, lat_rows)
@@ -61,13 +61,13 @@
     def w2_copy(t):
         return pltpu.make_async_copy(w2_hbm.at[t], w2.at[t], w2_sem)
 
-    for i in range(4):
+    for i in range(rows):
         lat_copy(i).start()
     lax.fori_loop(1, n_view, greet, 0, unroll=n_view <= 16)
     for t in range(9):
-        w1_copy(t).start()
+        w1_copy(t).start(priority=1)
     for i in range(4):
-        small_copy(i).start()
+        small_copy(i).start(priority=1)
 
     tiles = chans // TILE
     eye = (
@@ -94,7 +94,7 @@
     def prepare_all():
         pltpu.make_async_copy(w1.at[pl.ds(0, 5)], w1.at[pl.ds(0, 5)], w1_sem.at[0]).wait()
         for t in range(9):
-            w2_copy(t).start()
+            w2_copy(t).start(priority=1)
         pltpu.make_async_copy(w1.at[pl.ds(5, 4)], w1.at[pl.ds(5, 4)], w1_sem.at[1]).wait()
         lax.fori_loop(0, tiles * tiles, prepare, 0)
 
@@ -164,6 +164,14 @@
     def _():
         prepare_all()
 
+    zeros = jnp.zeros((edge.shape[1], 8, LANES), F32)
+
+    def clear(k, carry):
+        edge[k, :, pl.ds(0, 8)] = zeros
+        edge[k, :, pl.ds(cols + 8, 8)] = zeros
+        return carry
+
+    lax.fori_loop(0, edge.shape[0], clear, 0)
     pltpu.make_async_copy(w2, w2, w2_sem).wait()
 
     def fold_tile(j, carry):
@@ -225,15 +233,10 @@
     half_offset = offset * 0.5
 
     groups = range(chans // LANES)
-    first_row = lax.broadcasted_iota(jnp.int32, (8, LANES), 0)
-
-    def left_of(x):
-        y = pltpu.roll(x, 1, 0)
-        return jnp.concatenate([jnp.where(first_row == 0, 0.0, y[:8]), y[8:]], axis=0)
-
-    def right_of(x):
-        y = pltpu.roll(x, cols - 1, 0)
-        return jnp.concatenate([y[:-8], jnp.where(first_row == 7, 0.0, y[-8:])], axis=0)
+
+    def beside(slot, g, x):
+        edge[slot, g, pl.ds(8, cols)] = x
+        return edge[slot, g, pl.ds(7, cols)], edge[slot, g, pl.ds(9, cols)]
 
     def activate(i):
         for g in groups:
@@ -245,9 +248,10 @@
                 a = jnp.where(has_up, a, 0.0)
             if i >= rows + 2:
                 a = jnp.where(has_down, a, 0.0)
-            act[0, i, :, lanes] = left_of(a).astype(BF16)
+            left, right = beside(i, g, a)
+            act[0, i, :, lanes] = left.astype(BF16)
             act[1, i, :, lanes] = a.astype(BF16)
-            act[2, i, :, lanes] = right_of(a).astype(BF16)
+            act[2, i, :, lanes] = right.astype(BF16)
 
     inner = list(range(1, rows // 2))
     outer = [0, rows // 2]
@@ -284,9 +288,10 @@
             narrow = m.astype(BF16)
             m = narrow.astype(F32)
             to = pl.ds(i * cols, cols)
+            left, right = beside(rows + 4 + i, g, m)
             mx[0, to, lanes] = narrow
-            mx[1, to, lanes] = left_of(m).astype(BF16) - narrow
-            mx[2, to, lanes] = right_of(m).astype(BF16) - narrow
+            mx[1, to, lanes] = left.astype(BF16) - narrow
+            mx[2, to, lanes] = right.astype(BF16) - narrow
 
     def rise_of(n, j):
         lanes = pl.ds(n * TILE, TILE)
@@ -424,9 +429,10 @@
             pltpu.VMEM((3, own + cols, chans), BF16),
             pltpu.VMEM((chans // TILE, 2, own, TILE), F32),
             pltpu.VMEM((TILE // LANES, own * 4, LANES), F32),
+            pltpu.VMEM((2 * rows + 6, chans // LANES, cols + 16, LANES), F32),
             pltpu.VMEM((n_stat, LANES), F32),
             pltpu.VMEM((n_view - 1, n_stat, LANES), F32),
-            pltpu.SemaphoreType.DMA((4,)),
+            pltpu.SemaphoreType.DMA((rows,)),
             pltpu.SemaphoreType.DMA,
             pltpu.SemaphoreType.DMA((2,)),
             pltpu.SemaphoreType.DMA,

time: 16.6 us -> 16.5 us (level)
  no operation moved by 1% of the time
where the time goes in v4:
time: 16.5 us; the launch traced here: 16.4 us
  Pallas kernels  15 us (91%)
  local copies, waits for them, and re-layouts  1.32 us (8%)
    pallas_call x1, Pallas kernels, per_device(): pl.pallas_call(functools.partial(kernel, n_view, rows, cols, chans), out_...  15 us
    unnamed x1, local copies, waits for them, and re-layouts  1.32 us

profile of v4, /device:TPU:0, one launch (start us, length us, event | category | flops | bytes accessed | tf_op | source)
XLA Modules:
  0.0 16.4 jit_solution(2549277165701423598)
XLA Ops:
  0.0 15.0 %shard_map.73 = bf16[8,2,128,512]{3,2,1,0:T(8,128)(2,1)S(1)} custom-call(bf16[8,64,512]{2,1,0:T(8,128)(2,1)} %lat_hbm.1, f32[1,512]{1,0:T(1,128)} %bitcast.14, f32[1,512]{1,0:T(1,128)} %bitcast.15, bf16[9,512,512]{2,1,0:T(8,128)(2,1)} %bitcast.12, f32[1,512]{1,0:T(1,128)} %bitcast.16, bf16[9,512,512]{2,1,0:T(8,128)(2,1)} %bitcast.13, f32[1,512]{1,0:T(1,128)} %bitcast.17), custom_call_target="tpu_custom_call" | custom-call | tf_op jit(solution)/shard_map/pallas_call | solution.py:413
  15.0 1.3 %copy.9 = bf16[16,128,512]{2,1,0:T(8,128)(2,1)} copy(bf16[16,128,512]{2,1,0:T(8,128)(2,1)S(1)} %bitcast.11) | data formatting | bytes 4194304

commit v5 on v4

--- a/solution.py
+++ b/solution.py
@@ -363,6 +363,7 @@
 
     own_up.wait()
     own_down.wait()
+    finish(0, 0, [(2, rows - 3)])
     for i in (0, rows + 2):
         activate(i)
     arrange(0, outer)
@@ -378,7 +379,7 @@
         if n:
             for i in (0, 1, rows, rows + 1):
                 mix(n - 1, i)
-    finish(0, 0, [(2, rows - 3)])
+    finish(0, 1, [(1, rows - 3)])
     for i in (0, 1, rows, rows + 1):
         mix(columns[-1], i)
     for n in columns:
@@ -387,7 +388,7 @@
     for n in columns:
         level(n, [(0, 1), (rows - 1, 1)])
     finish(0, 0, [(0, 2), (rows - 1, 1)])
-    finish(0, 1, [(0, rows)])
+    finish(0, 1, [(0, 1), (rows - 2, 2)])
     for n in columns[1:]:
         finish(n, 0, [(0, rows)])
         finish(n, 1, [(0, rows)])

time: 16.5 us -> 16.5 us (level)
  no operation moved by 1% of the time
where the time goes in v5:
time: 16.5 us; the launch traced here: 16.3 us
  Pallas kernels  15 us (91%)
  local copies, waits for them, and re-layouts  1.32 us (8%)
    pallas_call x1, Pallas kernels, per_device(): pl.pallas_call(functools.partial(kernel, n_view, rows, cols, chans), out_...  15 us
    unnamed x1, local copies, waits for them, and re-layouts  1.32 us

profile of v5, /device:TPU:0, one launch (start us, length us, event | category | flops | bytes accessed | tf_op | source)
XLA Modules:
  0.0 16.3 jit_solution(10443363259661008122)
XLA Ops:
  0.0 15.0 %shard_map.73 = bf16[8,2,128,512]{3,2,1,0:T(8,128)(2,1)S(1)} custom-call(bf16[8,64,512]{2,1,0:T(8,128)(2,1)} %lat_hbm.1, f32[1,512]{1,0:T(1,128)} %bitcast.14, f32[1,512]{1,0:T(1,128)} %bitcast.15, bf16[9,512,512]{2,1,0:T(8,128)(2,1)} %bitcast.12, f32[1,512]{1,0:T(1,128)} %bitcast.16, bf16[9,512,512]{2,1,0:T(8,128)(2,1)} %bitcast.13, f32[1,512]{1,0:T(1,128)} %bitcast.17), custom_call_target="tpu_custom_call" | custom-call | tf_op jit(solution)/shard_map/pallas_call | solution.py:414
  15.0 1.3 %copy.9 = bf16[16,128,512]{2,1,0:T(8,128)(2,1)} copy(bf16[16,128,512]{2,1,0:T(8,128)(2,1)S(1)} %bitcast.11) | data formatting | bytes 4194304

commit v6 on v4

--- a/solution.py
+++ b/solution.py
@@ -29,10 +29,11 @@
     lat_hbm, gain_hbm, shift_hbm, w1_hbm, b1_hbm, w2_hbm, b2_hbm,
     out_ref,
     lat, small, w1, gt, w2, fold, act, vbuf, mbuf, mx, lhs_u, part, wide, edge, stat, stat_in,
-    lat_sem, small_sem, w1_sem, w2_sem, halo_send, halo_recv, stat_send, stat_recv,
+    lat_sem, small_sem, w1_sem, w2_sem, halo_send, halo_recv, stat_send, stat_recv, ready, paired,
 ):
     me = lax.axis_index("view")
     slabs = H_LAT // rows
+    assert slabs == 4
     views = n_view // slabs
     slab = me // views
     own = rows * cols
@@ -41,9 +42,41 @@
 
     barrier = pltpu.get_barrier_semaphore()
 
-    def greet(k, carry):
-        pl.semaphore_signal(barrier, inc=1, device_id={"view": lax.rem(me + k, n_view)})
+    hub = n_view - 2
+    above, below = me - views, me + views
+    first, second, third, last = slab == 0, slab == 1, slab == 2, slab == 3
+    between = jnp.logical_or(second, third)
+    rest = n_view - views
+    unrolled = n_view <= 16
+
+    def signal(to, carry=0):
+        @pl.when(to != me)
+        def _():
+            pl.semaphore_signal(barrier, inc=1, device_id={"view": to})
         return carry
+
+    def greet():
+        lax.fori_loop(rest, n_view, signal, 0, unroll=unrolled)
+
+        @pl.when(second)
+        def _():
+            signal(above)
+            signal(below)
+
+        @pl.when(first)
+        def _():
+            lax.fori_loop(views, rest, signal, 0, unroll=unrolled)
+
+    def spread_word():
+        @pl.when(me == hub)
+        def _():
+            pl.semaphore_wait(barrier, n_view - 1)
+
+            def tell(to, carry):
+                pl.semaphore_signal(ready, inc=1, device_id={"view": to})
+                return carry
+
+            lax.fori_loop(0, rest, tell, 0, unroll=unrolled)
 
     lat_rows = 1
 
@@ -63,7 +96,8 @@
 
     for i in range(rows):
         lat_copy(i).start()
-    lax.fori_loop(1, n_view, greet, 0, unroll=n_view <= 16)
+    greet()
+    spread_word()
     for t in range(9):
         w1_copy(t).start(priority=1)
     for i in range(4):
@@ -113,52 +147,80 @@
         [v[:, k * LANES : (k + 1) * LANES] for v in (sums, squares) for k in range(blocks)], axis=0
     )
 
-    @pl.when(jnp.logical_not(has_up))
-    def _():
-        prepare_all()
-
-    pl.semaphore_wait(barrier, n_view - 1)
-
-    def send_stat(k, carry):
-        to = k + (k >= me).astype(jnp.int32)
-        slot = lax.rem(to - me + n_view, n_view) - 1
-        pltpu.make_async_remote_copy(
-            src_ref=stat, dst_ref=stat_in.at[slot], send_sem=stat_send, recv_sem=stat_recv,
-            device_id={"view": to},
-        ).start()
-        return carry
-
-    lax.fori_loop(0, n_view - 1, send_stat, 0, unroll=n_view <= 16)
-
     up_copy = pltpu.make_async_remote_copy(
         src_ref=lat.at[pl.ds(2, 2)], dst_ref=lat.at[pl.ds(rows + 2, 2)],
         send_sem=halo_send.at[0], recv_sem=halo_recv.at[0],
-        device_id={"view": jnp.maximum(me - views, 0)},
+        device_id={"view": jnp.maximum(above, 0)},
     )
     down_copy = pltpu.make_async_remote_copy(
         src_ref=lat.at[pl.ds(rows, 2)], dst_ref=lat.at[pl.ds(0, 2)],
         send_sem=halo_send.at[1], recv_sem=halo_recv.at[1],
-        device_id={"view": jnp.minimum(me + views, n_view - 1)},
+        device_id={"view": jnp.minimum(below, n_view - 1)},
     )
-
     own_up = pltpu.make_async_copy(lat_hbm.at[pl.ds(0, 2)], lat.at[pl.ds(0, 2)], halo_recv.at[1])
     own_down = pltpu.make_async_copy(lat_hbm.at[pl.ds(0, 2)], lat.at[pl.ds(rows + 2, 2)], halo_recv.at[0])
 
-    @pl.when(has_up)
-    def _():
-        up_copy.start()
-
-    @pl.when(jnp.logical_not(has_up))
-    def _():
-        own_up.start()
-
-    @pl.when(has_down)
-    def _():
-        down_copy.start()
-
-    @pl.when(jnp.logical_not(has_down))
-    def _():
-        own_down.start()
+    def send_halos(*pairs):
+        for when, copy in pairs:
+            @pl.when(when)
+            def _():
+                copy.start()
+
+    def send_stat(to, carry):
+        @pl.when(to != me)
+        def _():
+            slot = lax.rem(to - me + n_view, n_view) - 1
+            pltpu.make_async_remote_copy(
+                src_ref=stat, dst_ref=stat_in.at[slot], send_sem=stat_send, recv_sem=stat_recv,
+                device_id={"view": to},
+            ).start()
+        return carry
+
+    @pl.when(first)
+    def _():
+        pl.semaphore_wait(barrier, 1)
+
+    @pl.when(third)
+    def _():
+        pl.semaphore_wait(barrier, views + 1)
+        pl.semaphore_signal(paired, inc=1, device_id={"view": above})
+
+    @pl.when(second)
+    def _():
+        pl.semaphore_wait(barrier, views)
+
+    @pl.when(between)
+    def _():
+        lax.fori_loop(0, views, send_stat, 0, unroll=unrolled)
+
+    send_halos((first, own_up), (first, down_copy), (between, up_copy))
+
+    @pl.when(second)
+    def _():
+        pl.semaphore_wait(paired, 1)
+
+    send_halos((second, down_copy))
+
+    @pl.when(first)
+    def _():
+        prepare_all()
+
+    @pl.when(jnp.logical_not(last))
+    def _():
+        pl.semaphore_wait(ready, 1)
+
+    @pl.when(jnp.logical_and(last, me != hub))
+    def _():
+        pl.semaphore_wait(barrier, n_view - 1)
+
+    @pl.when(jnp.logical_not(between))
+    def _():
+        lax.fori_loop(0, views, send_stat, 0, unroll=unrolled)
+
+    lax.fori_loop(views, n_view, send_stat, 0, unroll=unrolled)
+    send_halos(
+        (last, up_copy), (third, down_copy), (last, own_down)
+    )
 
     @pl.when(has_up)
     def _():
@@ -253,9 +315,8 @@
             act[1, i, :, lanes] = a.astype(BF16)
             act[2, i, :, lanes] = right.astype(BF16)
 
-    inner = list(range(1, rows // 2))
-    outer = [0, rows // 2]
-    place = {p: k for k, p in enumerate(inner + outer)}
+    pairs = list(range(rows // 2 + 1))
+    place = {p: p for p in pairs}
 
     def arrange(k, pairs):
         a, b = ((0, 2), (1, 2), (2, 1), (1, 3))[k]
@@ -340,57 +401,34 @@
 
     for i in range(2, rows + 2, 2):
         activate(i)
-    arrange(0, inner)
+
+    own_up.wait()
+    own_down.wait()
+    for i in (0, rows + 2):
+        activate(i)
+    arrange(0, pairs)
     for n in columns:
-        products(n, 0, inner)
-    for i in range(3, rows + 2, 2):
+        products(n, 0, pairs)
+    for i in range(1, rows + 4, 2):
         activate(i)
     for n in columns:
         for k in range(1, 4):
             if n == 0:
-                arrange(k, inner)
-            products(n, k, inner)
+                arrange(k, pairs)
+            products(n, k, pairs)
         if n:
-            for i in range(2, rows):
+            for i in range(rows + 2):
                 mix(n - 1, i)
-    for i in range(2, rows):
+    for i in range(rows + 2):
         mix(columns[-1], i)
     for n in columns:
-        level(n, [(1, rows - 2)])
+        level(n, [(0, rows)])
     for n in columns:
-        for j in range(2, rows - 1):
-            rise_of(n, j)
-
-    own_up.wait()
-    own_down.wait()
-    for i in (0, rows + 2):
-        activate(i)
-    arrange(0, outer)
-    for n in columns:
-        products(n, 0, outer)
-    for i in (1, rows + 3):
-        activate(i)
-    for n in columns:
-        for k in range(1, 4):
-            if n == 0:
-                arrange(k, outer)
-            products(n, k, outer)
-        if n:
-            for i in (0, 1, rows, rows + 1):
-                mix(n - 1, i)
-    finish(0, 0, [(2, rows - 3)])
-    for i in (0, 1, rows, rows + 1):
-        mix(columns[-1], i)
-    for n in columns:
-        for j in (0, 1, rows - 1, rows):
+        for j in range(rows + 1):
             rise_of(n, j)
     for n in columns:
-        level(n, [(0, 1), (rows - 1, 1)])
-    finish(0, 0, [(0, 2), (rows - 1, 1)])
-    finish(0, 1, [(0, rows)])
-    for n in columns[1:]:
-        finish(n, 0, [(0, rows)])
-        finish(n, 1, [(0, rows)])
+        for p in range(2):
+            finish(n, p, [(0, rows)])
 
     pltpu.make_async_copy(stat_in, stat_in, stat_send).wait()
 
@@ -440,6 +478,8 @@
             pltpu.SemaphoreType.DMA((2,)),
             pltpu.SemaphoreType.DMA,
             pltpu.SemaphoreType.DMA,
+            pltpu.SemaphoreType.REGULAR,
+            pltpu.SemaphoreType.REGULAR,
         ],
         compiler_params=pltpu.CompilerParams(
             collective_id=0, has_side_effects=True, vmem_limit_bytes=60 * 1024 * 1024

time: 16.5 us -> 16.4 us (level)
  no operation moved by 1% of the time
where the time goes in v6:
time: 16.4 us; the launch traced here: 16.2 us
  Pallas kernels  14.9 us (91%)
  local copies, waits for them, and re-layouts  1.32 us (8%)
    pallas_call x1, Pallas kernels, per_device(): pl.pallas_call(functools.partial(kernel, n_view, rows, cols, chans), out_...  14.9 us
    unnamed x1, local copies, waits for them, and re-layouts  1.32 us

profile of v6, /device:TPU:0, one launch (start us, length us, event | category | flops | bytes accessed | tf_op | source)
XLA Modules:
  0.0 16.2 jit_solution(18006030115421984033)
XLA Ops:
  0.0 14.9 %shard_map.73 = bf16[8,2,128,512]{3,2,1,0:T(8,128)(2,1)S(1)} custom-call(bf16[8,64,512]{2,1,0:T(8,128)(2,1)} %lat_hbm.1, f32[1,512]{1,0:T(1,128)} %bitcast.14, f32[1,512]{1,0:T(1,128)} %bitcast.15, bf16[9,512,512]{2,1,0:T(8,128)(2,1)} %bitcast.12, f32[1,512]{1,0:T(1,128)} %bitcast.16, bf16[9,512,512]{2,1,0:T(8,128)(2,1)} %bitcast.13, f32[1,512]{1,0:T(1,128)} %bitcast.17), custom_call_target="tpu_custom_call" | custom-call | tf_op jit(solution)/shard_map/pallas_call | solution.py:451
  14.9 1.3 %copy.9 = bf16[16,128,512]{2,1,0:T(8,128)(2,1)} copy(bf16[16,128,512]{2,1,0:T(8,128)(2,1)S(1)} %bitcast.11) | data formatting | bytes 4194304

commit v7 on v6

--- a/solution.py
+++ b/solution.py
@@ -28,7 +28,7 @@
     n_view, rows, cols, chans,
     lat_hbm, gain_hbm, shift_hbm, w1_hbm, b1_hbm, w2_hbm, b2_hbm,
     out_ref,
-    lat, small, w1, gt, w2, fold, act, vbuf, mbuf, mx, lhs_u, part, wide, edge, stat, stat_in,
+    lat, small, w1, gt, w2, fold, act, vbuf, mbuf, mx, lhs_u, part, wide, edge, raised, stat, stat_in,
     lat_sem, small_sem, w1_sem, w2_sem, halo_send, halo_recv, stat_send, stat_recv, ready, paired,
 ):
     me = lax.axis_index("view")
@@ -265,6 +265,12 @@
     lax.fori_loop(0, tiles * tiles, fold_tile, 0)
     pltpu.make_async_copy(small, small, small_sem).wait()
 
+    def raise_row(i, carry):
+        raised[i] = lat[2 + i].astype(F32) + small[2]
+        return carry
+
+    lax.fori_loop(0, rows, raise_row, 0)
+
     same = (
         lax.broadcasted_iota(jnp.int32, (LANES, LANES), 0) // (chans // GROUPS)
         == lax.broadcasted_iota(jnp.int32, (LANES, LANES), 1) // (chans // GROUPS)
@@ -282,8 +288,8 @@
     n_stat = 2 * blocks
     total = sized[:n_stat] + sized[n_stat : 2 * n_stat] + sized[2 * n_stat : 3 * n_stat]
     entries = float(own * (chans // GROUPS) * n_view)
-    mean = total[:blocks] / entries
-    var = total[blocks:] / entries - mean * mean
+    mean = total[:blocks] * (1.0 / entries)
+    var = total[blocks:] * (1.0 / entries) - mean * mean
     inv = lax.rsqrt(var + EPSILON)
 
     def one_row(v):
@@ -341,7 +347,10 @@
             lanes = pl.ds(g * LANES, LANES)
             v = [mbuf[k, at, lanes] for k in ((1, 2, 3) if odd else (0, 1, 2))]
             conv = v[0] - v[1] - v[2] if odd else v[0] + v[1] + v[2]
-            m = lat[i + 1, :, lanes].astype(F32) + conv + bias1[:, g * LANES : (g + 1) * LANES]
+            if 1 <= i <= rows:
+                m = raised[i - 1, :, lanes] + conv
+            else:
+                m = lat[i + 1, :, lanes].astype(F32) + conv + bias1[:, g * LANES : (g + 1) * LANES]
             if i == 0:
                 m = jnp.where(has_up, m, 0.0)
             if i == rows + 1:
@@ -412,7 +421,7 @@
     for i in range(1, rows + 4, 2):
         activate(i)
     for n in columns:
-        for k in range(1, 4):
+        for k in (3, 1, 2):
             if n == 0:
                 arrange(k, pairs)
             products(n, k, pairs)
@@ -422,11 +431,10 @@
     for i in range(rows + 2):
         mix(columns[-1], i)
     for n in columns:
-        level(n, [(0, rows)])
-    for n in columns:
         for j in range(rows + 1):
             rise_of(n, j)
     for n in columns:
+        level(n, [(0, rows)])
         for p in range(2):
             finish(n, p, [(0, rows)])
 
@@ -468,6 +476,7 @@
             pltpu.VMEM((chans // TILE, 2, own, TILE), F32),
             pltpu.VMEM((TILE // LANES, own * 4, LANES), F32),
             pltpu.VMEM((2 * rows + 6, chans // LANES, cols + 16, LANES), F32),
+            pltpu.VMEM((rows, cols, chans), F32),
             pltpu.VMEM((n_stat, LANES), F32),
             pltpu.VMEM((n_view - 1, n_stat, LANES), F32),
             pltpu.SemaphoreType.DMA((rows,)),

time: 16.4 us -> 16.2 us (0.988)
  Pallas kernels: 14.9 us -> 14.7 us
    pallas_call x1, Pallas kernels: 14.9 us -> 14.7 us  [per_device(): pl.pallas_call(functools.partial(kernel, n_view, rows, cols, chans), out_...]
where the time goes in v7:
time: 16.2 us; the launch traced here: 16.1 us
  Pallas kernels  14.7 us (91%)
  local copies, waits for them, and re-layouts  1.32 us (8%)
    pallas_call x1, Pallas kernels, per_device(): pl.pallas_call(functools.partial(kernel, n_view, rows, cols, chans), out_...  14.7 us
    unnamed x1, local copies, waits for them, and re-layouts  1.32 us

profile of v7, /device:TPU:0, one launch (start us, length us, event | category | flops | bytes accessed | tf_op | source)
XLA Modules:
  0.0 16.1 jit_solution(7732892132880932383)
XLA Ops:
  0.0 14.7 %shard_map.73 = bf16[8,2,128,512]{3,2,1,0:T(8,128)(2,1)S(1)} custom-call(bf16[8,64,512]{2,1,0:T(8,128)(2,1)} %lat_hbm.1, f32[1,512]{1,0:T(1,128)} %bitcast.14, f32[1,512]{1,0:T(1,128)} %bitcast.15, bf16[9,512,512]{2,1,0:T(8,128)(2,1)} %bitcast.12, f32[1,512]{1,0:T(1,128)} %bitcast.16, bf16[9,512,512]{2,1,0:T(8,128)(2,1)} %bitcast.13, f32[1,512]{1,0:T(1,128)} %bitcast.17), custom_call_target="tpu_custom_call" | custom-call | tf_op jit(solution)/shard_map/pallas_call | solution.py:459
  14.7 1.3 %copy.9 = bf16[16,128,512]{2,1,0:T(8,128)(2,1)} copy(bf16[16,128,512]{2,1,0:T(8,128)(2,1)S(1)} %bitcast.11) | data formatting | bytes 4194304

commit v8 on v7

--- a/solution.py
+++ b/solution.py
@@ -408,12 +408,12 @@
 
     columns = range(chans // width)
 
-    for i in range(2, rows + 2, 2):
+    for i in range(2, 6, 2):
         activate(i)
 
     own_up.wait()
     own_down.wait()
-    for i in (0, rows + 2):
+    for i in (0, *range(6, rows + 4, 2)):
         activate(i)
     arrange(0, pairs)
     for n in columns:

time: 16.2 us -> 16.1 us (level)
  no operation moved by 1% of the time
where the time goes in v8:
time: 16.1 us; the launch traced here: 16 us
  Pallas kernels  14.7 us (91%)
  local copies, waits for them, and re-layouts  1.32 us (8%)
    pallas_call x1, Pallas kernels, per_device(): pl.pallas_call(functools.partial(kernel, n_view, rows, cols, chans), out_...  14.7 us
    unnamed x1, local copies, waits for them, and re-layouts  1.32 us

profile of v8, /device:TPU:0, one launch (start us, length us, event | category | flops | bytes accessed | tf_op | source)
XLA Modules:
  0.0 16.0 jit_solution(6911030742859874714)
XLA Ops:
  0.0 14.7 %shard_map.73 = bf16[8,2,128,512]{3,2,1,0:T(8,128)(2,1)S(1)} custom-call(bf16[8,64,512]{2,1,0:T(8,128)(2,1)} %lat_hbm.1, f32[1,512]{1,0:T(1,128)} %bitcast.14, f32[1,512]{1,0:T(1,128)} %bitcast.15, bf16[9,512,512]{2,1,0:T(8,128)(2,1)} %bitcast.12, f32[1,512]{1,0:T(1,128)} %bitcast.16, bf16[9,512,512]{2,1,0:T(8,128)(2,1)} %bitcast.13, f32[1,512]{1,0:T(1,128)} %bitcast.17), custom_call_target="tpu_custom_call" | custom-call | tf_op jit(solution)/shard_map/pallas_call | solution.py:459
  14.7 1.3 %copy.9 = bf16[16,128,512]{2,1,0:T(8,128)(2,1)} copy(bf16[16,128,512]{2,1,0:T(8,128)(2,1)S(1)} %bitcast.11) | data formatting | bytes 4194304

commit v9 on v8

--- a/solution.py
+++ b/solution.py
@@ -408,12 +408,12 @@
 
     columns = range(chans // width)
 
-    for i in range(2, 6, 2):
+    for i in range(2, 4, 2):
         activate(i)
 
     own_up.wait()
     own_down.wait()
-    for i in (0, *range(6, rows + 4, 2)):
+    for i in (0, *range(4, rows + 4, 2)):
         activate(i)
     arrange(0, pairs)
     for n in columns:

time: 16.1 us -> 16.1 us (level)
  no operation moved by 1% of the time
where the time goes in v9:
time: 16.1 us; the launch traced here: 16 us
  Pallas kernels  14.6 us (91%)
  local copies, waits for them, and re-layouts  1.32 us (8%)
    pallas_call x1, Pallas kernels, per_device(): pl.pallas_call(functools.partial(kernel, n_view, rows, cols, chans), out_...  14.6 us
    unnamed x1, local copies, waits for them, and re-layouts  1.32 us

profile of v9, /device:TPU:0, one launch (start us, length us, event | category | flops | bytes accessed | tf_op | source)
XLA Modules:
  0.0 16.0 jit_solution(1306182883269711570)
XLA Ops:
  0.0 14.6 %shard_map.73 = bf16[8,2,128,512]{3,2,1,0:T(8,128)(2,1)S(1)} custom-call(bf16[8,64,512]{2,1,0:T(8,128)(2,1)} %lat_hbm.1, f32[1,512]{1,0:T(1,128)} %bitcast.14, f32[1,512]{1,0:T(1,128)} %bitcast.15, bf16[9,512,512]{2,1,0:T(8,128)(2,1)} %bitcast.12, f32[1,512]{1,0:T(1,128)} %bitcast.16, bf16[9,512,512]{2,1,0:T(8,128)(2,1)} %bitcast.13, f32[1,512]{1,0:T(1,128)} %bitcast.17), custom_call_target="tpu_custom_call" | custom-call | tf_op jit(solution)/shard_map/pallas_call | solution.py:459
  14.7 1.3 %copy.9 = bf16[16,128,512]{2,1,0:T(8,128)(2,1)} copy(bf16[16,128,512]{2,1,0:T(8,128)(2,1)S(1)} %bitcast.11) | data formatting | bytes 4194304

commit v10 on v7

--- a/solution.py
+++ b/solution.py
@@ -408,11 +408,11 @@
 
     columns = range(chans // width)
 
+    own_up.wait()
+    own_down.wait()
     for i in range(2, rows + 2, 2):
         activate(i)
 
-    own_up.wait()
-    own_down.wait()
     for i in (0, rows + 2):
         activate(i)
     arrange(0, pairs)

time: 16.2 us -> 16.2 us (level)
  no operation moved by 1% of the time
where the time goes in v10:
time: 16.2 us; the launch traced here: 16 us
  Pallas kernels  14.7 us (91%)
  local copies, waits for them, and re-layouts  1.32 us (8%)
    pallas_call x1, Pallas kernels, per_device(): pl.pallas_call(functools.partial(kernel, n_view, rows, cols, chans), out_...  14.7 us
    unnamed x1, local copies, waits for them, and re-layouts  1.32 us

profile of v10, /device:TPU:0, one launch (start us, length us, event | category | flops | bytes accessed | tf_op | source)
XLA Modules:
  0.0 16.0 jit_solution(10453900638513290019)
XLA Ops:
  0.0 14.7 %shard_map.73 = bf16[8,2,128,512]{3,2,1,0:T(8,128)(2,1)S(1)} custom-call(bf16[8,64,512]{2,1,0:T(8,128)(2,1)} %lat_hbm.1, f32[1,512]{1,0:T(1,128)} %bitcast.14, f32[1,512]{1,0:T(1,128)} %bitcast.15, bf16[9,512,512]{2,1,0:T(8,128)(2,1)} %bitcast.12, f32[1,512]{1,0:T(1,128)} %bitcast.16, bf16[9,512,512]{2,1,0:T(8,128)(2,1)} %bitcast.13, f32[1,512]{1,0:T(1,128)} %bitcast.17), custom_call_target="tpu_custom_call" | custom-call | tf_op jit(solution)/shard_map/pallas_call | solution.py:459
  14.7 1.3 %copy.9 = bf16[16,128,512]{2,1,0:T(8,128)(2,1)} copy(bf16[16,128,512]{2,1,0:T(8,128)(2,1)S(1)} %bitcast.11) | data formatting | bytes 4194304
